TPU v7x, 32 devices: a whole 2x2x4 slice. The times are simulated.
32 devices in a mesh: samp: 16 (over z, y, x), feat: 2 (over core).
Axes of the slice: x: 2, y: 2, z: 4, core: 2. Of those that a mesh axis runs over, the one named last changes fastest.
Arguments:
- design_matrix: bfloat16 [2048, 32768], P('samp', 'feat'), may hold values from -0.046875 to 0.046875
- labels: int32 [2048], P('samp'), may hold values from 0 to 1
- weights: float32 [16, 32768], P(None, ('feat', 'samp')), may hold values from -6 to 6
- lambdas: float32 [16], replicated, may hold values from 0.05 to 1
- sketch: bfloat16 [32768, 384], P(('feat', 'samp')), may hold values from -0.03125 to 0.03125
- sketch_values: float32 [384], replicated, may hold values from 0.05 to 2
Outputs:
- new_weights: float32 [16, 32768], P(None, ('feat', 'samp'))
All inputs are finite; a program needn't handle non-finite values.
Results may differ from a plain program's by a relative error of at most 0.004.
Values may be sent and summed in bfloat16 or wider, within the bound.
No kernel may reach another device: no remote copies, remote signals or barrier semaphores. Data moves between devices by JAX's collectives and lax.ppermute only.
A program may use at most 64 MiB of HBM per device.

v0:
```python
import jax
import jax.numpy as jnp
from jax import lax
from jax.sharding import PartitionSpec as P

ITERS = 2


def shards(design_matrix, labels, weights, lambdas, sketch, sketch_values):
    sketch_full = sketch.astype(jnp.float32)
    smallest = jnp.min(sketch_values)
    ratios = (smallest + lambdas[:, None]) / (sketch_values[None, :] + lambdas[:, None]) - 1.0

    def apply_rows(vector):
        vector_half = vector.astype(jnp.bfloat16)
        partial_rows = lax.dot_general(
            lax.all_gather(vector_half, "samp", axis=1, tiled=True),
            design_matrix,
            (((1,), (1,)), ((), ())),
            preferred_element_type=jnp.float32,
        )
        return lax.psum(partial_rows, "feat")

    def apply_columns(values):
        return lax.psum_scatter(
            lax.dot_general(
                design_matrix, values, (((0,), (1,)), ((), ())), preferred_element_type=jnp.float32
            ),
            "samp",
            scatter_dimension=0,
            tiled=True,
        ).T

    def precondition(residual):
        projected = jnp.dot(residual, sketch_full, precision=lax.Precision.HIGHEST)
        projected = lax.psum(projected, ("samp", "feat"))
        correction = lax.dot_general(
            ratios * projected,
            sketch_full,
            (((1,), (1,)), ((), ())),
            precision=lax.Precision.HIGHEST,
        )
        precond_res = residual + correction
        res_dot = lax.psum(jnp.sum(residual * precond_res, axis=1), ("samp", "feat"))
        return (precond_res, res_dot)

    logits = apply_rows(weights)
    probability = jax.nn.sigmoid(logits)
    hessian_diag = probability * (1.0 - probability)
    miss_rows = (probability - labels[None, :].astype(jnp.float32)).astype(jnp.bfloat16)
    gradient = apply_columns(miss_rows) + lambdas[:, None] * weights
    residual = -gradient
    precond_res, res_dot = precondition(residual)
    direction = precond_res
    update = jnp.zeros_like(residual)
    for iteration in range(ITERS):
        image_rows = apply_rows(direction)
        hess_dir = (
            apply_columns((hessian_diag * image_rows).astype(jnp.bfloat16))
            + lambdas[:, None] * direction
        )
        curvature = lax.psum(jnp.sum(direction * hess_dir, axis=1), ("samp", "feat"))
        step_size = res_dot / curvature
        update = update + step_size[:, None] * direction
        if iteration + 1 < ITERS:
            residual = residual - step_size[:, None] * hess_dir
            precond_res, new_dot = precondition(residual)
            direction = precond_res + (new_dot / res_dot)[:, None] * direction
            res_dot = new_dot
    return weights + update


def solution(mesh):
    return jax.shard_map(
        shards,
        mesh=mesh,
        in_specs=(
            P("samp", "feat"),
            P("samp"),
            P(None, ("feat", "samp")),
            P(),
            P(("feat", "samp"), None),
            P(),
        ),
        out_specs=P(None, ("feat", "samp")),
        check_vma=False,
    )
```

profile of v0, /device:TPU:10, one launch (start us, length us, event | category | flops | bytes accessed | tf_op | source)
XLA Modules:
  0.0 596.1 jit_solution(18189731865618623638)
XLA Ops:
  8.1 33.0 %all_gather.9 = bf16[16,16384]{1,0:T(8,128)(2,1)S(1)} all-gather(bf16[16,1024]{1,0:T(8,128)(2,1)S(1)} %convert_element_type.23), channel_id=1, replica_groups=mesh['samp'=16,'feat'=2] {'samp'}, dimensions={1}, use_global_device_ids=true | all-gather | bytes 557056 | tf_op jit(solution)/shard_map/all_gather | solution.py:17
  41.1 3.4 fusion.22
  44.5 2.6 psum.63
  47.1 3.8 convolution_bitcast_fusion.2
  52.3 73.3 %reduce-scatter.4.cloned.1.call-done = f32[1024,16]{0,1:T(8,128)} async-done(((f32[16384,16]{0,1:T(8,128)}), f32[1024,16]{0,1:T(8,128)}) %reduce-scatter.4.cloned.1.call-update) | async-done | bytes 65552 | tf_op jit(solution)/shard_map/reduce_scatter | solution.py:25
  125.6 0.9 fusion.2
  127.0 50.1 %psum.64 = f32[16,384]{1,0:T(8,128)S(1)} all-reduce(f32[16,384]{1,0:T(8,128)S(1)} %fusion.23), channel_id=1, replica_groups=mesh['samp'=16,'feat'=2] {'samp','feat'}, use_global_device_ids=true, to_apply=%region_3.0 | all-reduce | flops 6144 | bytes 49152 | tf_op jit(solution)/shard_map/psum | solution.py:36
  177.8 32.0 %all_gather.10 = bf16[16,16384]{1,0:T(8,128)(2,1)S(1)} all-gather(bf16[16,1024]{1,0:T(8,128)(2,1)S(1)} %get-tuple-element.9), channel_id=1, replica_groups=mesh['samp'=16,'feat'=2] {'samp'}, dimensions={1}, use_global_device_ids=true | all-gather | bytes 557056 | tf_op jit(solution)/shard_map/all_gather | solution.py:17
  209.8 3.4 fusion.24
  213.1 2.5 psum.66
  215.6 3.8 convolution_bitcast_fusion.1
  219.5 71.6 %reduce-scatter.6.cloned.1.call-done = f32[1024,16]{0,1:T(8,128)} async-done(((f32[16384,16]{0,1:T(8,128)}), f32[1024,16]{0,1:T(8,128)}) %reduce-scatter.6.cloned.1.call-update) | async-done | bytes 65552 | tf_op jit(solution)/shard_map/reduce_scatter | solution.py:25
  291.1 1.0 multiply_reduce_fusion.1
  292.1 49.7 %all-reduce = (f32[16]{0:T(128)S(1)}, f32[16]{0:T(128)S(1)}) all-reduce(f32[16]{0:T(128)S(1)} %get-tuple-element.6, f32[16]{0:T(128)S(1)} %get-tuple-element.5), channel_id=1, replica_groups=mesh['samp'=16,'feat'=2] {'samp','feat'}, use_global_device_ids=true, to_apply=%region_5.0 | all-reduce | flops 32 | bytes 256 | tf_op jit(solution)/shard_map/psum | solution.py:44
  341.9 0.9 multiply_subtract_fusion
  343.2 38.3 %psum.68 = f32[16,384]{1,0:T(8,128)S(1)} all-reduce(f32[16,384]{1,0:T(8,128)S(1)} %fusion.25), channel_id=1, replica_groups=mesh['samp'=16,'feat'=2] {'samp','feat'}, use_global_device_ids=true, to_apply=%region_10.0 | all-reduce | flops 6144 | bytes 49152 | tf_op jit(solution)/shard_map/psum | solution.py:36
  382.3 41.9 %psum.69 = f32[16]{0:T(128)S(1)} all-reduce(f32[16]{0:T(128)S(1)} %get-tuple-element.11), channel_id=1, replica_groups=mesh['samp'=16,'feat'=2] {'samp','feat'}, use_global_device_ids=true, to_apply=%region_12.0 | all-reduce | flops 16 | bytes 128 | tf_op jit(solution)/shard_map/psum | solution.py:44
  424.3 31.8 %all_gather.11 = bf16[16,16384]{1,0:T(8,128)(2,1)S(1)} all-gather(bf16[16,1024]{1,0:T(8,128)(2,1)S(1)} %fusion.20), channel_id=1, replica_groups=mesh['samp'=16,'feat'=2] {'samp'}, dimensions={1}, use_global_device_ids=true | all-gather | bytes 557056 | tf_op jit(solution)/shard_map/all_gather | solution.py:17
  456.1 3.4 fusion.26
  459.5 2.5 psum.70
  462.0 3.9 convolution_bitcast_fusion
  465.8 72.2 %reduce-scatter.8.cloned.1.call-done = f32[1024,16]{0,1:T(8,128)} async-done(((f32[16384,16]{0,1:T(8,128)}), f32[1024,16]{0,1:T(8,128)}) %reduce-scatter.8.cloned.1.call-update) | async-done | bytes 65552 | tf_op jit(solution)/shard_map/reduce_scatter | solution.py:25
  538.1 1.0 fusion.1
  539.1 49.8 %psum.71 = f32[16]{0:T(128)S(1)} all-reduce(f32[16]{0:T(128)S(1)} %fusion.1), channel_id=1, replica_groups=mesh['samp'=16,'feat'=2] {'samp','feat'}, use_global_device_ids=true, to_apply=%region_16.0 | all-reduce | flops 16 | bytes 128 | tf_op jit(solution)/shard_map/psum | solution.py:62
  (27 shorter events, 6.2 us)
Async XLA Ops:
  6.5 120.0 %copy-start = (bf16[1024,384]{1,0:T(8,128)(2,1)S(1)}, bf16[1024,384]{1,0:T(8,128)(2,1)}, u32[]{:S(2)}) copy-start(bf16[1024,384]{1,0:T(8,128)(2,1)} %param.10) | copy-start | bytes 2359300
  6.5 119.1 %reduce-scatter.4.cloned.1.call-start = ((), (), s32[]{:S(2)}) async-start(), calls=%async_computation.3 | async-start | bytes 1114112 | tf_op jit(solution)/shard_map/reduce_scatter | solution.py:25
  44.4 6.6 %copy-start.3 = (f32[384]{0:T(512)S(1)}, f32[384]{0:T(512)}, u32[]{:S(2)}) copy-start(f32[384]{0:T(512)} %param.11) | copy-start | bytes 4612
  44.4 7.2 %copy-start.2 = (f32[16]{0:T(128)S(1)}, f32[16]{0:T(128)}, u32[]{:S(2)}) copy-start(f32[16]{0:T(128)} %param.9) | copy-start | bytes 196
  44.4 81.2 %copy-start.1 = (f32[16,1024]{1,0:T(8,128)S(1)}, f32[16,1024]{1,0:T(8,128)}, u32[]{:S(2)}) copy-start(f32[16,1024]{1,0:T(8,128)} %param.8) | copy-start | bytes 196612
  51.0 240.1 %reduce-scatter.6.cloned.1.call-start = ((), (), s32[]{:S(2)}) async-start(), calls=%async_computation.4 | async-start | bytes 1114112 | tf_op jit(solution)/shard_map/reduce_scatter | solution.py:25
  219.5 318.6 %reduce-scatter.8.cloned.1.call-start = ((), (), s32[]{:S(2)}) async-start(), calls=%async_computation.5 | async-start | bytes 1114112 | tf_op jit(solution)/shard_map/reduce_scatter | solution.py:25
Sparse Core Ops, SparseCore 0:
  51.1 74.4 reduce-scatter.3
  219.6 71.4 reduce-scatter.5
  466.0 72.0 reduce-scatter.7
where the time goes:
time: 597 us; the launch traced here: 596 us
  blocking collectives  334 us (56%)
  waiting for transfers between devices  217 us (36%)
  matrix products  24.1 us (4%)
  between operations  13.2 us (2%)
  other arithmetic  7.54 us (1%)
    reduce_scatter x3, waiting for transfers between devices, apply_columns(): lax.psum_scatter(lax.dot_general(design_matrix, values, (((0,), (1,)), ((...  217 us
    all_gather x3, blocking collectives, apply_rows(): lax.all_gather(vector_half, 'samp', axis=1, tiled=True)  96.7 us
    psum x2, blocking collectives, precondition(): lax.psum(jnp.sum(residual * precond_res, axis=1), ('samp', 'feat'))  91.6 us
    psum x2, blocking collectives, precondition(): projected = lax.psum(projected, ('samp', 'feat'))  88.3 us
    psum x1, blocking collectives, shards(): lax.psum(jnp.sum(direction * hess_dir, axis=1), ('samp', 'feat'))  49.8 us
  transfers between devices with their start and end apart: 3, of which 3 were waited for; matrix products, arithmetic and copies ran while one was open for 0% of the time, Pallas kernels for 0%

commit v1 on v0

--- a/solution.py
+++ b/solution.py
@@ -41,7 +41,7 @@
             precision=lax.Precision.HIGHEST,
         )
         precond_res = residual + correction
-        res_dot = lax.psum(jnp.sum(residual * precond_res, axis=1), ("samp", "feat"))
+        res_dot = lax.psum(lax.psum(jnp.sum(residual * precond_res, axis=1), "samp"), "feat")
         return (precond_res, res_dot)
 
     logits = apply_rows(weights)

time: 597 us -> 637 us (1.067)
  blocking collectives: 334 us -> 375 us
    psum x1 -> x2, blocking collectives: 49.8 us -> 99.5 us  [shards(): lax.psum(jnp.sum(direction * hess_dir, axis=1), ('samp', 'feat'))]
    psum x2 -> x4, blocking collectives: 91.6 us -> 63.1 us  [the longest x2 58.2 us: precondition(): lax.psum(jnp.sum(residual * precond_res, axis=1), 'samp')]
    psum x2, blocking collectives: 88.3 us -> 98 us  [precondition(): projected = lax.psum(projected, ('samp', 'feat'))]
    all_gather x3, blocking collectives: 96.7 us -> 106 us  [apply_rows(): lax.all_gather(vector_half, 'samp', axis=1, tiled=True)]
where the time goes in v1:
time: 637 us; the launch traced here: 636 us
  blocking collectives  375 us (59%)
  waiting for transfers between devices  217 us (34%)
  matrix products  24.1 us (4%)
  between operations  13.2 us (2%)
  other arithmetic  7.54 us (1%)
    reduce_scatter x3, waiting for transfers between devices, apply_columns(): lax.psum_scatter(lax.dot_general(design_matrix, values, (((0,), (1,)), ((...  216 us
    all_gather x3, blocking collectives, apply_rows(): lax.all_gather(vector_half, 'samp', axis=1, tiled=True)  106 us
    psum x2, blocking collectives, shards(): lax.psum(jnp.sum(direction * hess_dir, axis=1), ('samp', 'feat'))  99.5 us
    psum x2, blocking collectives, precondition(): projected = lax.psum(projected, ('samp', 'feat'))  98 us
    psum x2, blocking collectives, precondition(): lax.psum(jnp.sum(residual * precond_res, axis=1), 'samp')  58.2 us
  transfers between devices with their start and end apart: 3, of which 3 were waited for; matrix products, arithmetic and copies ran while one was open for 0% of the time, Pallas kernels for 0%

profile of v1, /device:TPU:10, one launch (start us, length us, event | category | flops | bytes accessed | tf_op | source)
XLA Modules:
  0.0 635.9 jit_solution(4179257262181225480)
XLA Ops:
  8.1 33.0 %all_gather.9 = bf16[16,16384]{1,0:T(8,128)(2,1)S(1)} all-gather(bf16[16,1024]{1,0:T(8,128)(2,1)S(1)} %convert_element_type.23), channel_id=1, replica_groups=mesh['samp'=16,'feat'=2] {'samp'}, dimensions={1}, use_global_device_ids=true | all-gather | bytes 557056 | tf_op jit(solution)/shard_map/all_gather | solution.py:17
  41.1 3.4 fusion.22
  44.5 2.6 psum.77
  47.1 3.8 convolution_bitcast_fusion.2
  52.3 73.3 %reduce-scatter.4.cloned.1.call-done = f32[1024,16]{0,1:T(8,128)} async-done(((f32[16384,16]{0,1:T(8,128)}), f32[1024,16]{0,1:T(8,128)}) %reduce-scatter.4.cloned.1.call-update) | async-done | bytes 65552 | tf_op jit(solution)/shard_map/reduce_scatter | solution.py:25
  127.0 50.1 %psum.78 = f32[16,384]{1,0:T(8,128)S(1)} all-reduce(f32[16,384]{1,0:T(8,128)S(1)} %fusion.23), channel_id=1, replica_groups=mesh['samp'=16,'feat'=2] {'samp','feat'}, use_global_device_ids=true, to_apply=%region_3.0 | all-reduce | flops 6144 | bytes 49152 | tf_op jit(solution)/shard_map/psum | solution.py:36
  177.8 32.0 %all_gather.10 = bf16[16,16384]{1,0:T(8,128)(2,1)S(1)} all-gather(bf16[16,1024]{1,0:T(8,128)(2,1)S(1)} %get-tuple-element.7), channel_id=1, replica_groups=mesh['samp'=16,'feat'=2] {'samp'}, dimensions={1}, use_global_device_ids=true | all-gather | bytes 557056 | tf_op jit(solution)/shard_map/all_gather | solution.py:17
  209.8 3.4 fusion.24
  213.1 2.5 psum.81
  215.6 3.8 convolution_bitcast_fusion.1
  219.5 71.6 %reduce-scatter.6.cloned.1.call-done = f32[1024,16]{0,1:T(8,128)} async-done(((f32[16384,16]{0,1:T(8,128)}), f32[1024,16]{0,1:T(8,128)}) %reduce-scatter.6.cloned.1.call-update) | async-done | bytes 65552 | tf_op jit(solution)/shard_map/reduce_scatter | solution.py:25
  292.1 49.7 %psum.82 = f32[16]{0:T(128)S(1)} all-reduce(f32[16]{0:T(128)S(1)} %get-tuple-element.5), channel_id=1, replica_groups=mesh['samp'=16,'feat'=2] {'samp','feat'}, use_global_device_ids=true, to_apply=%region_10.0 | all-reduce | flops 16 | bytes 128 | tf_op jit(solution)/shard_map/psum | solution.py:62
  341.8 29.1 %psum.79 = f32[16]{0:T(128)S(1)} all-reduce(f32[16]{0:T(128)S(1)} %get-tuple-element.6), channel_id=1, replica_groups=mesh['samp'=16,'feat'=2] {'samp'}, use_global_device_ids=true, to_apply=%region_5.0 | all-reduce | flops 16 | bytes 128 | tf_op jit(solution)/shard_map/psum | solution.py:44
  370.9 2.5 psum.80
  374.7 47.9 %psum.83 = f32[16,384]{1,0:T(8,128)S(1)} all-reduce(f32[16,384]{1,0:T(8,128)S(1)} %fusion.25), channel_id=1, replica_groups=mesh['samp'=16,'feat'=2] {'samp','feat'}, use_global_device_ids=true, to_apply=%region_11.0 | all-reduce | flops 6144 | bytes 49152 | tf_op jit(solution)/shard_map/psum | solution.py:36
  423.5 29.1 %psum.84 = f32[16]{0:T(128)S(1)} all-reduce(f32[16]{0:T(128)S(1)} %get-tuple-element.9), channel_id=1, replica_groups=mesh['samp'=16,'feat'=2] {'samp'}, use_global_device_ids=true, to_apply=%region_13.0 | all-reduce | flops 16 | bytes 128 | tf_op jit(solution)/shard_map/psum | solution.py:44
  452.7 2.5 psum.85
  455.2 41.4 %all_gather.11 = bf16[16,16384]{1,0:T(8,128)(2,1)S(1)} all-gather(bf16[16,1024]{1,0:T(8,128)(2,1)S(1)} %fusion.20), channel_id=1, replica_groups=mesh['samp'=16,'feat'=2] {'samp'}, dimensions={1}, use_global_device_ids=true | all-gather | bytes 557056 | tf_op jit(solution)/shard_map/all_gather | solution.py:17
  496.6 3.4 fusion.26
  499.9 2.5 psum.86
  502.4 3.9 convolution_bitcast_fusion
  506.3 71.6 %reduce-scatter.8.cloned.1.call-done = f32[1024,16]{0,1:T(8,128)} async-done(((f32[16384,16]{0,1:T(8,128)}), f32[1024,16]{0,1:T(8,128)}) %reduce-scatter.8.cloned.1.call-update) | async-done | bytes 65552 | tf_op jit(solution)/shard_map/reduce_scatter | solution.py:25
  577.9 1.0 fusion.1
  578.9 49.8 %psum.87 = f32[16]{0:T(128)S(1)} all-reduce(f32[16]{0:T(128)S(1)} %fusion.1), channel_id=1, replica_groups=mesh['samp'=16,'feat'=2] {'samp','feat'}, use_global_device_ids=true, to_apply=%region_18.0 | all-reduce | flops 16 | bytes 128 | tf_op jit(solution)/shard_map/psum | solution.py:62
  (30 shorter events, 9.1 us)
Async XLA Ops:
  6.5 120.0 %copy-start = (bf16[1024,384]{1,0:T(8,128)(2,1)S(1)}, bf16[1024,384]{1,0:T(8,128)(2,1)}, u32[]{:S(2)}) copy-start(bf16[1024,384]{1,0:T(8,128)(2,1)} %param.10) | copy-start | bytes 2359300
  6.5 119.1 %reduce-scatter.4.cloned.1.call-start = ((), (), s32[]{:S(2)}) async-start(), calls=%async_computation.3 | async-start | bytes 1114112 | tf_op jit(solution)/shard_map/reduce_scatter | solution.py:25
  44.4 6.6 %copy-start.3 = (f32[384]{0:T(512)S(1)}, f32[384]{0:T(512)}, u32[]{:S(2)}) copy-start(f32[384]{0:T(512)} %param.11) | copy-start | bytes 4612
  44.4 7.2 %copy-start.2 = (f32[16]{0:T(128)S(1)}, f32[16]{0:T(128)}, u32[]{:S(2)}) copy-start(f32[16]{0:T(128)} %param.9) | copy-start | bytes 196
  44.4 81.2 %copy-start.1 = (f32[16,1024]{1,0:T(8,128)S(1)}, f32[16,1024]{1,0:T(8,128)}, u32[]{:S(2)}) copy-start(f32[16,1024]{1,0:T(8,128)} %param.8) | copy-start | bytes 196612
  51.0 240.1 %reduce-scatter.6.cloned.1.call-start = ((), (), s32[]{:S(2)}) async-start(), calls=%async_computation.4 | async-start | bytes 1114112 | tf_op jit(solution)/shard_map/reduce_scatter | solution.py:25
  219.5 358.4 %reduce-scatter.8.cloned.1.call-start = ((), (), s32[]{:S(2)}) async-start(), calls=%async_computation.5 | async-start | bytes 1114112 | tf_op jit(solution)/shard_map/reduce_scatter | solution.py:25
Sparse Core Ops, SparseCore 0:
  51.1 74.4 reduce-scatter.3
  219.6 71.4 reduce-scatter.5
  506.4 71.4 reduce-scatter.7
